TPU v7x, 512 devices: a whole 4x8x8 slice. The times are simulated.
512 devices in a mesh: col: 64 (over y_hi, x, z), tok: 8 (over y_lo, core).
Axes of the slice: x: 4, y: 8 (y_hi: 2, y_lo: 4; y = y_hi * 4 + y_lo), z: 8, core: 2. Of those that a mesh axis runs over, the one named last changes fastest.
Arguments:
- acts: bfloat16 [2048, 8192], P('tok', 'col'), may hold values from -6 to 6
- grad_out: bfloat16 [2048, 8192], P('tok', 'col'), may hold values from -0.19921875 to 0.19921875
- left_factor: float32 [8, 8192, 1024], P('tok', 'col'), may hold values from -6 to 6
- right_factor: float32 [8, 8192, 1024], P('tok', 'col'), may hold values from -6 to 6
- left_basis: bfloat16 [8, 8192, 1024], P('tok', 'col'), may hold values from -0.1875 to 0.1875
- right_basis: bfloat16 [8, 8192, 1024], P('tok', 'col'), may hold values from -0.1875 to 0.1875
- moment: float32 [8192, 8192], P('tok', 'col'), may hold values from -2 to 2
- second: float32 [8192, 8192], P('tok', 'col'), may hold values from 0.05 to 2
Outputs:
- left_out: float32 [8, 8192, 1024], P('tok', 'col')
- right_out: float32 [8, 8192, 1024], P('tok', 'col')
- moment_out: float32 [8192, 8192], P('tok', 'col')
- second_out: float32 [8192, 8192], P('tok', 'col')
- update: bfloat16 [8192, 8192], P('tok', 'col')
All inputs are finite; a program needn't handle non-finite values.
Results may differ from a plain program's by a relative error of at most 0.0075.
Values may be sent and summed in bfloat16 or wider, within the bound.
A program may use at most 64 MiB of HBM per device.

v0:
```python
import jax
import jax.numpy as jnp
from jax import lax
from jax.sharding import PartitionSpec as P

B = 1024
shampoo_beta = 0.95
first_beta = 0.9
second_beta = 0.95
first_corr = 1.0 - 0.9**4
second_corr = 1.0 - 0.95**4
epsilon = 1e-08


def swapped(array, axis, distance):
    return lax.ppermute(array, axis, [(i, i ^ 1 << distance) for i in range(lax.axis_size(axis))])


def join_pair(current, incoming, axis, lower):
    width = current.shape[axis]
    shape = list(current.shape)
    shape[axis] = 2 * width
    joined = jnp.zeros(shape, current.dtype)
    mine_at = jnp.where(lower, 0, width)
    theirs_at = width - mine_at
    joined = lax.dynamic_update_slice_in_dim(joined, current, mine_at, axis)
    return lax.dynamic_update_slice_in_dim(joined, incoming, theirs_at, axis)


def shards(acts, grad_out, left_factor, right_factor, left_basis, right_basis, moment, second):
    width = grad_out.shape[1]
    blocks = left_factor.shape[0]
    groups = B // width
    nbits = groups.bit_length() - 1
    member = lax.axis_index("col") % groups
    contract = (((0,), (0,)), ((), ()))
    term = lax.dot_general(
        lax.all_gather(acts, "col", axis=1, tiled=True),
        grad_out,
        contract,
        preferred_element_type=jnp.float32,
    )
    grad = lax.psum_scatter(term, "tok", scatter_dimension=0, tiled=True)
    own = grad.astype(jnp.bfloat16).reshape(blocks, B, width)
    tiles, left_full, right_full = (own, left_basis, right_basis)
    for bit in range(nbits):
        other = swapped((tiles, left_full, right_full), "col", bit)
        lower = member >> bit & 1 == 0
        tiles = join_pair(tiles, other[0], 2, lower)
        left_full = join_pair(left_full, other[1], 1, lower)
        right_full = join_pair(right_full, other[2], 1, lower)
    right_cols = lax.dynamic_slice_in_dim(right_full, member * width, width, 2)
    mixed = jnp.einsum(
        "nab,nbc->nac", tiles, right_cols, preferred_element_type=jnp.float32
    ).astype(jnp.bfloat16)
    lead = lax.dynamic_slice_in_dim(tiles, member * width, width, 1)
    left_new = shampoo_beta * left_factor + (1.0 - shampoo_beta) * jnp.einsum(
        "nab,ncb->nac", lead, tiles, preferred_element_type=jnp.float32
    )
    right_new = shampoo_beta * right_factor + (1.0 - shampoo_beta) * jnp.einsum(
        "nat,nab->ntb", own, tiles, preferred_element_type=jnp.float32
    )
    rotated = jnp.einsum("nab,nac->nbc", left_full, mixed, preferred_element_type=jnp.float32)
    first_new = first_beta * moment.reshape(blocks, B, width) + (1.0 - first_beta) * rotated
    second_new = (
        second_beta * second.reshape(blocks, B, width) + (1.0 - second_beta) * rotated * rotated
    )
    normed = (first_new / first_corr / (jnp.sqrt(second_new / second_corr) + epsilon)).astype(
        jnp.bfloat16
    )
    steps_full = normed
    for bit in range(nbits):
        other_steps = swapped(steps_full, "col", bit)
        lower = member >> bit & 1 == 0
        steps_full = join_pair(steps_full, other_steps, 2, lower)
    back = jnp.einsum(
        "nab,ncb->nac", steps_full, right_basis, preferred_element_type=jnp.float32
    ).astype(jnp.bfloat16)
    update = jnp.einsum("nab,nbc->nac", left_full, back, preferred_element_type=jnp.float32).astype(
        jnp.bfloat16
    )
    rows = blocks * B
    return (
        left_new,
        right_new,
        first_new.reshape(rows, width),
        second_new.reshape(rows, width),
        update.reshape(rows, width),
    )


def solution(mesh):
    in_specs = (
        P("tok", "col"),
        P("tok", "col"),
        P("tok", "col", None),
        P("tok", "col", None),
        P("tok", "col", None),
        P("tok", "col", None),
        P("tok", "col"),
        P("tok", "col"),
    )
    out_specs = (
        P("tok", "col", None),
        P("tok", "col", None),
        P("tok", "col"),
        P("tok", "col"),
        P("tok", "col"),
    )
    return jax.shard_map(shards, mesh=mesh, in_specs=in_specs, out_specs=out_specs, check_vma=False)
```

profile of v0, /device:TPU:9, one launch (start us, length us, event | category | flops | bytes accessed | tf_op | source)
XLA Modules:
  0.0 488.8 jit_solution(3307319483804612024)
XLA Ops:
  7.2 0.7 all-gather.2.cloned.1.call-update
  8.0 126.3 %all-gather.2.cloned.1.call-done = bf16[256,8192]{1,0:T(8,128)(2,1)} async-done(((bf16[256,128]{1,0:T(8,128)(2,1)}), bf16[256,8192]{1,0:T(8,128)(2,1)}) %all-gather.2.cloned.1.call-update) | async-done | bytes 4194320 | tf_op jit(solution)/shard_map/all_gather | solution.py:38
  134.3 5.4 %fusion.50 = f32[8192,128]{1,0:T(8,128)} fusion(bf16[256,8192]{1,0:T(8,128)(2,1)} %all-gather.2.cloned.1.call-done, bf16[256,128]{1,0:T(8,128)(2,1)S(1)} %copy-done), kind=kOutput, calls=%fused_computation.54 | convolution fusion | flops 536870912 | bytes 8454144 | tf_op jit(solution)/shard_map/dot_general | solution.py:37
  139.7 0.9 copy-done.7
  140.7 1.9 collective-permute-start.6
  142.6 3.4 collective-permute-start.3
  146.1 1.7 collective-permute-done.6
  147.8 2.3 collective-permute-start.7
  150.2 2.5 collective-permute-done.3
  152.7 1.9 collective-permute-start.4
  154.6 44.9 %reduce-scatter.2.cloned.1.call-done = f32[1024,128]{1,0:T(8,128)} async-done(((f32[8192,128]{1,0:T(8,128)}), f32[1024,128]{1,0:T(8,128)}) %reduce-scatter.2.cloned.1.call-update) | async-done | bytes 524304 | tf_op jit(solution)/shard_map/reduce_scatter | solution.py:43
  199.6 0.8 broadcast.41.clone
  200.4 1.9 constant_dynamic-update-slice_fusion.19
  202.3 3.2 collective-permute-start
  205.6 0.1 broadcast.44.clone.1
  205.8 6.8 %collective-permute-start.8 = (bf16[1,512,1024]{2,1,0:T(8,128)(2,1)S(1)}, bf16[1,512,1024]{2,1,0:T(8,128)(2,1)}, u32[]{:S(2)}, u32[]{:S(2)}) collective-permute-start(bf16[1,512,1024]{2,1,0:T(8,128)(2,1)S(1)} %constant_dynamic-update-slice_fusion.6), channel_id=1, source_target_pairs={{0,32},{8,40},{16,48},{24,56},{32,0},{40,8},{48,16},{56,24},{64,96... | collective-permute-start | bytes 3145736 | tf_op jit(solution)/shard_map/ppermute | solution.py:16
  212.7 1.7 constant_dynamic-update-slice_fusion.18
  214.3 3.4 collective-permute-start.1
  217.8 0.1 broadcast.44.clone
  218.0 7.8 %collective-permute-start.5 = (bf16[1,512,1024]{2,1,0:T(8,128)(2,1)S(1)}, bf16[1,512,1024]{2,1,0:T(8,128)(2,1)}, u32[]{:S(2)}, u32[]{:S(2)}) collective-permute-start(bf16[1,512,1024]{2,1,0:T(8,128)(2,1)S(1)} %constant_dynamic-update-slice_fusion.10), channel_id=1, source_target_pairs={{0,32},{8,40},{16,48},{24,56},{32,0},{40,8},{48,16},{56,24},{64,96... | collective-permute-start | bytes 3145736 | tf_op jit(solution)/shard_map/ppermute | solution.py:16
  225.8 0.1 broadcast.40.clone
  225.9 1.1 constant_dynamic-update-slice_fusion.17
  227.0 100.2 %collective-permute-done.1 = bf16[1,1024,256]{2,1,0:T(8,128)(2,1)S(1)} collective-permute-done((bf16[1,1024,256]{2,1,0:T(8,128)(2,1)}, bf16[1,1024,256]{2,1,0:T(8,128)(2,1)S(1)}, u32[]{:S(2)}, u32[]{:S(2)}) %collective-permute-start.1) | collective-permute-done | bytes 524320 | tf_op jit(solution)/shard_map/ppermute | solution.py:16
  327.2 5.2 %collective-permute-start.2 = (bf16[1,1024,512]{2,1,0:T(8,128)(2,1)S(1)}, bf16[1,1024,512]{2,1,0:T(8,128)(2,1)}, u32[]{:S(2)}, u32[]{:S(2)}) collective-permute-start(bf16[1,1024,512]{2,1,0:T(8,128)(2,1)S(1)} %constant_dynamic-update-slice_fusion.16), channel_id=1, source_target_pairs={{0,32},{8,40},{16,48},{24,56},{32,0},{40,8},{48,16},{56,24},{64,96... | collective-permute-start | bytes 3145736 | tf_op jit(solution)/shard_map/ppermute | solution.py:16
  332.4 0.3 broadcast.39.clone.1
  332.6 0.1 constant_dynamic-update-slice_fusion.5
  332.8 0.3 broadcast.43.clone
  333.0 0.1 bitcast_dynamic-update-slice_fusion.3
  333.2 1.3 constant_dynamic-update-slice_fusion.4
  334.5 2.1 bitcast_dynamic-update-slice_fusion.2
  336.6 0.3 broadcast.39.clone
  336.9 0.2 constant_dynamic-update-slice_fusion.15
  337.1 0.9 copy-done.2
  337.9 42.3 %collective-permute-done.2 = bf16[1,1024,512]{2,1,0:T(8,128)(2,1)} collective-permute-done((bf16[1,1024,512]{2,1,0:T(8,128)(2,1)S(1)}, bf16[1,1024,512]{2,1,0:T(8,128)(2,1)}, u32[]{:S(2)}, u32[]{:S(2)}) %collective-permute-start.2) | collective-permute-done | bytes 1048608 | tf_op jit(solution)/shard_map/ppermute | solution.py:16
  380.3 1.4 constant_dynamic-update-slice_fusion.14
  381.7 5.3 %constant_dynamic-update-slice_fusion.3 = (bf16[1,1024,256]{2,1,0:T(8,128)(2,1)S(1)}, bf16[1,1024,128]{2,1,0:T(8,128)(2,1)S(1)}, f32[1024,128]{1,0:T(8,128)}, f32[1024,128]{1,0:T(8,128)}) fusion(bf16[1,1024,256]{2,1,0:T(8,128)(2,1)S(1)} %broadcast.41, s32[]{:T(128)S(6)} %select_n.61, f32[1024,128]{1,0:T(8,128)} %param.15, f32[1024,128]{1,0:T(8,128)} %param.14, ...), kind=kOutput, calls=%fused_computation.35 | convolution fusion | flops 538574848 | bytes 7077896 | tf_op jit(solution)/shard_map/nab,nac->nbc/dot_general | solution.py:63
  387.1 2.0 collective-permute-start.9
  389.1 7.0 %collective-permute-done.9 = bf16[1,1024,128]{2,1,0:T(8,128)(2,1)S(1)} collective-permute-done((bf16[1,1024,128]{2,1,0:T(8,128)(2,1)S(1)}, bf16[1,1024,128]{2,1,0:T(8,128)(2,1)S(1)}, u32[]{:S(2)}, u32[]{:S(2)}) %collective-permute-start.9) | collective-permute-done | bytes 262176 | tf_op jit(solution)/shard_map/ppermute | solution.py:16
  396.1 2.8 collective-permute-start.10
  399.1 24.9 %collective-permute-done.10 = bf16[1,1024,256]{2,1,0:T(8,128)(2,1)S(1)} collective-permute-done((bf16[1,1024,256]{2,1,0:T(8,128)(2,1)S(1)}, bf16[1,1024,256]{2,1,0:T(8,128)(2,1)S(1)}, u32[]{:S(2)}, u32[]{:S(2)}) %collective-permute-start.10) | collective-permute-done | bytes 524320 | tf_op jit(solution)/shard_map/ppermute | solution.py:16
  424.0 5.1 %collective-permute-start.11 = (bf16[1,1024,512]{2,1,0:T(8,128)(2,1)S(1)}, bf16[1,1024,512]{2,1,0:T(8,128)(2,1)S(1)}, u32[]{:S(2)}, u32[]{:S(2)}) collective-permute-start(bf16[1,1024,512]{2,1,0:T(8,128)(2,1)S(1)} %constant_dynamic-update-slice_fusion), channel_id=1, source_target_pairs={{0,32},{8,40},{16,48},{24,56},{32,0},{40,8},{48,16},{56,24},{64,96... | collective-permute-start | bytes 3145736 | tf_op jit(solution)/shard_map/ppermute | solution.py:16
  429.2 1.6 fusion.21
  430.8 1.3 fusion.18
  432.1 0.3 broadcast.43
  432.3 0.1 bitcast_dynamic-update-slice_fusion.1
  432.5 44.8 %collective-permute-done.11 = bf16[1,1024,512]{2,1,0:T(8,128)(2,1)S(1)} collective-permute-done((bf16[1,1024,512]{2,1,0:T(8,128)(2,1)S(1)}, bf16[1,1024,512]{2,1,0:T(8,128)(2,1)S(1)}, u32[]{:S(2)}, u32[]{:S(2)}) %collective-permute-start.11) | collective-permute-done | bytes 1048608 | tf_op jit(solution)/shard_map/ppermute | solution.py:16
  477.3 0.1 bitcast_dynamic-update-slice_fusion
  477.5 4.5 convolution_convert_fusion
  (38 shorter events, 0.8 us)
Async XLA Ops:
  7.2 127.1 %copy-start = (bf16[256,128]{1,0:T(8,128)(2,1)S(1)}, bf16[256,128]{1,0:T(8,128)(2,1)}, u32[]{:S(2)}) copy-start(bf16[256,128]{1,0:T(8,128)(2,1)} %param.9) | copy-start | bytes 196612
  7.2 127.1 %all-gather.2.cloned.1.call-start = ((), (), s32[]{:S(2)}) async-start(), calls=%async_computation.1 | async-start | bytes 4259840 | tf_op jit(solution)/shard_map/all_gather | solution.py:38
  7.9 191.7 %reduce-scatter.2.cloned.1.call-start = ((), (), s32[]{:S(2)}) async-start(), calls=%async_computation.2 | async-start | bytes 4718592 | tf_op jit(solution)/shard_map/reduce_scatter | solution.py:43
  139.7 0.9 copy-start.7
  139.7 2.9 copy-start.6
  140.7 7.1 %collective-permute-start.6 = (bf16[1,128,1024]{2,1,0:T(8,128)(2,1)S(1)}, bf16[1,128,1024]{2,1,0:T(8,128)(2,1)S(1)}, u32[]{:S(2)}, u32[]{:S(2)}) collective-permute-start(bf16[1,128,1024]{2,1,0:T(8,128)(2,1)S(1)} %copy-done.7), channel_id=1, source_target_pairs={{0,8},{8,0},{16,24},{24,16},{32,40},{40,32},{48,56},{56,48},{64,72... | collective-permute-start | bytes 786440 | tf_op jit(solution)/shard_map/ppermute | solution.py:16
  142.6 10.1 %collective-permute-start.3 = (bf16[1,128,1024]{2,1,0:T(8,128)(2,1)S(1)}, bf16[1,128,1024]{2,1,0:T(8,128)(2,1)S(1)}, u32[]{:S(2)}, u32[]{:S(2)}) collective-permute-start(bf16[1,128,1024]{2,1,0:T(8,128)(2,1)S(1)} %copy-done.6), channel_id=1, source_target_pairs={{0,8},{8,0},{16,24},{24,16},{32,40},{40,32},{48,56},{56,48},{64,72... | collective-permute-start | bytes 786440 | tf_op jit(solution)/shard_map/ppermute | solution.py:16
  147.8 58.0 %collective-permute-start.7 = (bf16[1,256,1024]{2,1,0:T(8,128)(2,1)S(1)}, bf16[1,256,1024]{2,1,0:T(8,128)(2,1)S(1)}, u32[]{:S(2)}, u32[]{:S(2)}) collective-permute-start(bf16[1,256,1024]{2,1,0:T(8,128)(2,1)S(1)} %constant_dynamic-update-slice_fusion.8), channel_id=1, source_target_pairs={{0,16},{8,24},{16,0},{24,8},{32,48},{40,56},{48,32},{56,40},{64,80... | collective-permute-start | bytes 1572872 | tf_op jit(solution)/shard_map/ppermute | solution.py:16
  152.7 65.3 %collective-permute-start.4 = (bf16[1,256,1024]{2,1,0:T(8,128)(2,1)S(1)}, bf16[1,256,1024]{2,1,0:T(8,128)(2,1)S(1)}, u32[]{:S(2)}, u32[]{:S(2)}) collective-permute-start(bf16[1,256,1024]{2,1,0:T(8,128)(2,1)S(1)} %constant_dynamic-update-slice_fusion.12), channel_id=1, source_target_pairs={{0,16},{8,24},{16,0},{24,8},{32,48},{40,56},{48,32},{56,40},{64,80... | collective-permute-start | bytes 1572872 | tf_op jit(solution)/shard_map/ppermute | solution.py:16
  202.3 10.4 %collective-permute-start = (bf16[1,1024,128]{2,1,0:T(8,128)(2,1)}, bf16[1,1024,128]{2,1,0:T(8,128)(2,1)}, u32[]{:S(2)}, u32[]{:S(2)}) collective-permute-start(bf16[1,1024,128]{2,1,0:T(8,128)(2,1)} %get-tuple-element.10), channel_id=1, source_target_pairs={{0,8},{8,0},{16,24},{24,16},{32,40},{40,32},{48,56},{56,48},{64,72... | collective-permute-start | bytes 786440 | tf_op jit(solution)/shard_map/ppermute | solution.py:16
  205.8 127.3 %collective-permute-start.8 = (bf16[1,512,1024]{2,1,0:T(8,128)(2,1)S(1)}, bf16[1,512,1024]{2,1,0:T(8,128)(2,1)}, u32[]{:S(2)}, u32[]{:S(2)}) collective-permute-start(bf16[1,512,1024]{2,1,0:T(8,128)(2,1)S(1)} %constant_dynamic-update-slice_fusion.6), channel_id=1, source_target_pairs={{0,32},{8,40},{16,48},{24,56},{32,0},{40,8},{48,16},{56,24},{64,96... | collective-permute-start | bytes 3145736 | tf_op jit(solution)/shard_map/ppermute | solution.py:16
  214.3 112.8 %collective-permute-start.1 = (bf16[1,1024,256]{2,1,0:T(8,128)(2,1)}, bf16[1,1024,256]{2,1,0:T(8,128)(2,1)S(1)}, u32[]{:S(2)}, u32[]{:S(2)}) collective-permute-start(bf16[1,1024,256]{2,1,0:T(8,128)(2,1)} %constant_dynamic-update-slice_fusion.18), channel_id=1, source_target_pairs={{0,16},{8,24},{16,0},{24,8},{32,48},{40,56},{48,32},{56,40},{64,80... | collective-permute-start | bytes 1572872 | tf_op jit(solution)/shard_map/ppermute | solution.py:16
  218.0 116.5 %collective-permute-start.5 = (bf16[1,512,1024]{2,1,0:T(8,128)(2,1)S(1)}, bf16[1,512,1024]{2,1,0:T(8,128)(2,1)}, u32[]{:S(2)}, u32[]{:S(2)}) collective-permute-start(bf16[1,512,1024]{2,1,0:T(8,128)(2,1)S(1)} %constant_dynamic-update-slice_fusion.10), channel_id=1, source_target_pairs={{0,32},{8,40},{16,48},{24,56},{32,0},{40,8},{48,16},{56,24},{64,96... | collective-permute-start | bytes 3145736 | tf_op jit(solution)/shard_map/ppermute | solution.py:16
  327.2 53.1 %collective-permute-start.2 = (bf16[1,1024,512]{2,1,0:T(8,128)(2,1)S(1)}, bf16[1,1024,512]{2,1,0:T(8,128)(2,1)}, u32[]{:S(2)}, u32[]{:S(2)}) collective-permute-start(bf16[1,1024,512]{2,1,0:T(8,128)(2,1)S(1)} %constant_dynamic-update-slice_fusion.16), channel_id=1, source_target_pairs={{0,32},{8,40},{16,48},{24,56},{32,0},{40,8},{48,16},{56,24},{64,96... | collective-permute-start | bytes 3145736 | tf_op jit(solution)/shard_map/ppermute | solution.py:16
  334.5 2.4 copy-start.1
  336.6 1.3 copy-start.2
  387.1 42.1 %copy-start.5 = (f32[1,128,1024]{2,1,0:T(8,128)S(1)}, f32[1,128,1024]{2,1,0:T(8,128)}, u32[]{:S(2)}) copy-start(f32[1,128,1024]{2,1,0:T(8,128)} %param.10) | copy-start | bytes 1572868
  387.1 9.0 %collective-permute-start.9 = (bf16[1,1024,128]{2,1,0:T(8,128)(2,1)S(1)}, bf16[1,1024,128]{2,1,0:T(8,128)(2,1)S(1)}, u32[]{:S(2)}, u32[]{:S(2)}) collective-permute-start(bf16[1,1024,128]{2,1,0:T(8,128)(2,1)S(1)} %get-tuple-element.6), channel_id=1, source_target_pairs={{0,8},{8,0},{16,24},{24,16},{32,40},{40,32},{48,56},{56,48},{64,72... | collective-permute-start | bytes 786440 | tf_op jit(solution)/shard_map/ppermute | solution.py:16
  396.1 27.9 %collective-permute-start.10 = (bf16[1,1024,256]{2,1,0:T(8,128)(2,1)S(1)}, bf16[1,1024,256]{2,1,0:T(8,128)(2,1)S(1)}, u32[]{:S(2)}, u32[]{:S(2)}) collective-permute-start(bf16[1,1024,256]{2,1,0:T(8,128)(2,1)S(1)} %constant_dynamic-update-slice_fusion.2), channel_id=1, source_target_pairs={{0,16},{8,24},{16,0},{24,8},{32,48},{40,56},{48,32},{56,40},{64,80... | collective-permute-start | bytes 1572872 | tf_op jit(solution)/shard_map/ppermute | solution.py:16
  399.1 31.7 %copy-start.3 = (f32[1024,128]{1,0:T(8,128)S(1)}, f32[1024,128]{1,0:T(8,128)}, u32[]{:S(2)}) copy-start(f32[1024,128]{1,0:T(8,128)} %reduce-scatter.2.cloned.1.call-done) | copy-start | bytes 1572868
  399.1 31.7 %copy-start.4 = (f32[1,128,1024]{2,1,0:T(8,128)S(1)}, f32[1,128,1024]{2,1,0:T(8,128)}, u32[]{:S(2)}) copy-start(f32[1,128,1024]{2,1,0:T(8,128)} %param.11) | copy-start | bytes 1572868
  424.0 53.3 %collective-permute-start.11 = (bf16[1,1024,512]{2,1,0:T(8,128)(2,1)S(1)}, bf16[1,1024,512]{2,1,0:T(8,128)(2,1)S(1)}, u32[]{:S(2)}, u32[]{:S(2)}) collective-permute-start(bf16[1,1024,512]{2,1,0:T(8,128)(2,1)S(1)} %constant_dynamic-update-slice_fusion), channel_id=1, source_target_pairs={{0,32},{8,40},{16,48},{24,56},{32,0},{40,8},{48,16},{56,24},{64,96... | collective-permute-start | bytes 3145736 | tf_op jit(solution)/shard_map/ppermute | solution.py:16
Sparse Core Ops, SparseCore 0:
  12.3 121.9 all-gather.1
  139.9 59.6 reduce-scatter.1
where the time goes:
time: 490 us; the launch traced here: 489 us
  waiting for transfers between devices  395 us (81%)
  starting transfers between devices  46 us (9%)
  matrix products  18.2 us (4%)
  between operations  14.5 us (3%)
  local copies, waits for them, and re-layouts  12.9 us (3%)
    ppermute x12, waiting for transfers between devices, swapped(): lax.ppermute(array, axis, [(i, i ^ 1 << distance) for i in range(lax.axis...  223 us
    all_gather x1, waiting for transfers between devices, shards(): lax.all_gather(acts, 'col', axis=1, tiled=True)  126 us
    ppermute x12, starting transfers between devices, swapped(): lax.ppermute(array, axis, [(i, i ^ 1 << distance) for i in range(lax.axis...  45.9 us
    reduce_scatter x1, waiting for transfers between devices, shards(): grad = lax.psum_scatter(term, 'tok', scatter_dimension=0, tiled=True)  44.9 us
  transfers between devices with their start and end apart: 14, of which 9 were waited for; matrix products, arithmetic and copies ran while one was open for 3% of the time, Pallas kernels for 0%

commit v1 on v0

--- a/solution.py
+++ b/solution.py
@@ -10,6 +10,13 @@
 first_corr = 1.0 - 0.9**4
 second_corr = 1.0 - 0.95**4
 epsilon = 1e-08
+
+
+def gather_over(x, axis, along):
+    size = lax.axis_size(axis)
+    blocks = jnp.stack([x for _ in range(size)])
+    blocks = lax.all_to_all(blocks, axis, split_axis=0, concat_axis=0)
+    return jnp.concatenate(blocks, axis=along)
 
 
 def swapped(array, axis, distance):
@@ -35,10 +42,7 @@
     member = lax.axis_index("col") % groups
     contract = (((0,), (0,)), ((), ()))
     term = lax.dot_general(
-        lax.all_gather(acts, "col", axis=1, tiled=True),
-        grad_out,
-        contract,
-        preferred_element_type=jnp.float32,
+        gather_over(acts, "col", 1), grad_out, contract, preferred_element_type=jnp.float32
     )
     grad = lax.psum_scatter(term, "tok", scatter_dimension=0, tiled=True)
     own = grad.astype(jnp.bfloat16).reshape(blocks, B, width)

time: 490 us -> 480 us (0.980)
  the two profiles are of different devices: /device:TPU:9 before, /device:TPU:11 now
where the time goes in v1:
time: 480 us; the launch traced here: 479 us
  waiting for transfers between devices  261 us (54%)
  blocking collectives  122 us (25%)
  starting transfers between devices  48.5 us (10%)
  matrix products  16 us (3%)
  between operations  14.5 us (3%)
  local copies, waits for them, and re-layouts  14.3 us (3%)
    ppermute x12, waiting for transfers between devices, swapped(): lax.ppermute(array, axis, [(i, i ^ 1 << distance) for i in range(lax.axis...  223 us
    all_to_all x1, blocking collectives, gather_over(): blocks = lax.all_to_all(blocks, axis, split_axis=0, concat_axis=0)  122 us
    ppermute x12, starting transfers between devices, swapped(): lax.ppermute(array, axis, [(i, i ^ 1 << distance) for i in range(lax.axis...  48.4 us
    reduce_scatter x1, waiting for transfers between devices, shards(): grad = lax.psum_scatter(term, 'tok', scatter_dimension=0, tiled=True)  38.1 us
  transfers between devices with their start and end apart: 13, of which 8 were waited for; matrix products, arithmetic and copies ran while one was open for 3% of the time, Pallas kernels for 0%

profile of v1, /device:TPU:11, one launch (start us, length us, event | category | flops | bytes accessed | tf_op | source)
XLA Modules:
  0.0 478.9 jit_solution(14204031253762432484)
XLA Ops:
  7.2 0.9 copy.13
  8.2 0.5 stack.2
  8.7 122.2 %all_to_all.5 = bf16[64,256,128]{1,2,0:T(8,128)(2,1)S(1)} all-to-all(bf16[64,256,128]{1,2,0:T(8,128)(2,1)S(1)} %stack.2), channel_id=1, replica_groups=mesh['col'=64,'tok'=8] {'col'}, dimensions={0} | all-to-all | bytes 8388608 | tf_op jit(solution)/shard_map/all_to_all | solution.py:18
  130.9 3.2 fusion.50
  134.1 0.9 copy-done.7
  135.1 3.3 collective-permute-start.6
  138.4 1.9 collective-permute-start.3
  140.5 3.0 collective-permute-done.6
  143.5 2.5 collective-permute-start.7
  146.1 3.1 collective-permute-done.3
  149.2 2.4 collective-permute-start.4
  151.6 38.1 %reduce-scatter.2.cloned.1.call-done = f32[1024,128]{1,0:T(8,128)} async-done(((f32[8192,128]{1,0:T(8,128)}), f32[1024,128]{1,0:T(8,128)}) %reduce-scatter.2.cloned.1.call-update) | async-done | bytes 524304 | tf_op jit(solution)/shard_map/reduce_scatter | solution.py:47
  189.8 0.8 broadcast.43.clone
  190.6 1.9 constant_dynamic-update-slice_fusion.19
  192.5 3.1 collective-permute-start
  195.6 0.1 broadcast.46.clone.1
  195.8 6.8 %collective-permute-start.8 = (bf16[1,512,1024]{2,1,0:T(8,128)(2,1)S(1)}, bf16[1,512,1024]{2,1,0:T(8,128)(2,1)}, u32[]{:S(2)}, u32[]{:S(2)}) collective-permute-start(bf16[1,512,1024]{2,1,0:T(8,128)(2,1)S(1)} %constant_dynamic-update-slice_fusion.6), channel_id=1, source_target_pairs={{0,32},{8,40},{16,48},{24,56},{32,0},{40,8},{48,16},{56,24},{64,96... | collective-permute-start | bytes 3145736 | tf_op jit(solution)/shard_map/ppermute | solution.py:23
  202.7 1.7 constant_dynamic-update-slice_fusion.18
  204.3 3.5 collective-permute-start.1
  207.8 0.1 broadcast.46.clone
  208.1 9.8 %collective-permute-start.5 = (bf16[1,512,1024]{2,1,0:T(8,128)(2,1)S(1)}, bf16[1,512,1024]{2,1,0:T(8,128)(2,1)}, u32[]{:S(2)}, u32[]{:S(2)}) collective-permute-start(bf16[1,512,1024]{2,1,0:T(8,128)(2,1)S(1)} %constant_dynamic-update-slice_fusion.10), channel_id=1, source_target_pairs={{0,32},{8,40},{16,48},{24,56},{32,0},{40,8},{48,16},{56,24},{64,96... | collective-permute-start | bytes 3145736 | tf_op jit(solution)/shard_map/ppermute | solution.py:23
  217.9 1.1 constant_dynamic-update-slice_fusion.17
  219.0 98.1 %collective-permute-done.1 = bf16[1,1024,256]{2,1,0:T(8,128)(2,1)S(1)} collective-permute-done((bf16[1,1024,256]{2,1,0:T(8,128)(2,1)}, bf16[1,1024,256]{2,1,0:T(8,128)(2,1)S(1)}, u32[]{:S(2)}, u32[]{:S(2)}) %collective-permute-start.1) | collective-permute-done | bytes 524320 | tf_op jit(solution)/shard_map/ppermute | solution.py:23
  317.2 5.2 %collective-permute-start.2 = (bf16[1,1024,512]{2,1,0:T(8,128)(2,1)S(1)}, bf16[1,1024,512]{2,1,0:T(8,128)(2,1)}, u32[]{:S(2)}, u32[]{:S(2)}) collective-permute-start(bf16[1,1024,512]{2,1,0:T(8,128)(2,1)S(1)} %constant_dynamic-update-slice_fusion.16), channel_id=1, source_target_pairs={{0,32},{8,40},{16,48},{24,56},{32,0},{40,8},{48,16},{56,24},{64,96... | collective-permute-start | bytes 3145736 | tf_op jit(solution)/shard_map/ppermute | solution.py:23
  322.4 0.3 broadcast.41.clone.1
  322.7 0.1 constant_dynamic-update-slice_fusion.5
  322.8 0.3 broadcast.45.clone
  323.0 0.1 bitcast_dynamic-update-slice_fusion.3
  323.2 1.3 constant_dynamic-update-slice_fusion.4
  324.5 2.1 bitcast_dynamic-update-slice_fusion.2
  326.6 0.3 broadcast.41.clone
  326.9 0.2 constant_dynamic-update-slice_fusion.15
  327.1 0.9 copy-done.2
  328.0 42.4 %collective-permute-done.2 = bf16[1,1024,512]{2,1,0:T(8,128)(2,1)} collective-permute-done((bf16[1,1024,512]{2,1,0:T(8,128)(2,1)S(1)}, bf16[1,1024,512]{2,1,0:T(8,128)(2,1)}, u32[]{:S(2)}, u32[]{:S(2)}) %collective-permute-start.2) | collective-permute-done | bytes 1048608 | tf_op jit(solution)/shard_map/ppermute | solution.py:23
  370.3 1.4 constant_dynamic-update-slice_fusion.14
  371.8 5.3 %constant_dynamic-update-slice_fusion.3 = (bf16[1,1024,256]{2,1,0:T(8,128)(2,1)S(1)}, bf16[1,1024,128]{2,1,0:T(8,128)(2,1)S(1)}, f32[1024,128]{1,0:T(8,128)}, f32[1024,128]{1,0:T(8,128)}) fusion(bf16[1,1024,256]{2,1,0:T(8,128)(2,1)S(1)} %broadcast.43, s32[]{:T(128)S(6)} %select_n.61, f32[1024,128]{1,0:T(8,128)} %param.15, f32[1024,128]{1,0:T(8,128)} %param.14, ...), kind=kOutput, calls=%fused_computation.35 | convolution fusion | flops 538574848 | bytes 7077896 | tf_op jit(solution)/shard_map/nab,nac->nbc/dot_general | solution.py:67
  377.1 2.0 collective-permute-start.9
  379.1 7.0 %collective-permute-done.9 = bf16[1,1024,128]{2,1,0:T(8,128)(2,1)S(1)} collective-permute-done((bf16[1,1024,128]{2,1,0:T(8,128)(2,1)S(1)}, bf16[1,1024,128]{2,1,0:T(8,128)(2,1)S(1)}, u32[]{:S(2)}, u32[]{:S(2)}) %collective-permute-start.9) | collective-permute-done | bytes 262176 | tf_op jit(solution)/shard_map/ppermute | solution.py:23
  386.2 2.8 collective-permute-start.10
  389.1 24.9 %collective-permute-done.10 = bf16[1,1024,256]{2,1,0:T(8,128)(2,1)S(1)} collective-permute-done((bf16[1,1024,256]{2,1,0:T(8,128)(2,1)S(1)}, bf16[1,1024,256]{2,1,0:T(8,128)(2,1)S(1)}, u32[]{:S(2)}, u32[]{:S(2)}) %collective-permute-start.10) | collective-permute-done | bytes 524320 | tf_op jit(solution)/shard_map/ppermute | solution.py:23
  414.1 5.1 %collective-permute-start.11 = (bf16[1,1024,512]{2,1,0:T(8,128)(2,1)S(1)}, bf16[1,1024,512]{2,1,0:T(8,128)(2,1)S(1)}, u32[]{:S(2)}, u32[]{:S(2)}) collective-permute-start(bf16[1,1024,512]{2,1,0:T(8,128)(2,1)S(1)} %constant_dynamic-update-slice_fusion), channel_id=1, source_target_pairs={{0,32},{8,40},{16,48},{24,56},{32,0},{40,8},{48,16},{56,24},{64,96... | collective-permute-start | bytes 3145736 | tf_op jit(solution)/shard_map/ppermute | solution.py:23
  419.2 1.6 fusion.21
  420.8 1.3 fusion.18
  422.1 0.3 broadcast.45
  422.4 0.1 bitcast_dynamic-update-slice_fusion.1
  422.5 44.9 %collective-permute-done.11 = bf16[1,1024,512]{2,1,0:T(8,128)(2,1)S(1)} collective-permute-done((bf16[1,1024,512]{2,1,0:T(8,128)(2,1)S(1)}, bf16[1,1024,512]{2,1,0:T(8,128)(2,1)S(1)}, u32[]{:S(2)}, u32[]{:S(2)}) %collective-permute-start.11) | collective-permute-done | bytes 1048608 | tf_op jit(solution)/shard_map/ppermute | solution.py:23
  467.4 0.1 bitcast_dynamic-update-slice_fusion
  467.5 4.5 convolution_convert_fusion
  (38 shorter events, 0.9 us)
Async XLA Ops:
  7.2 123.7 %copy-start = (bf16[256,128]{1,0:T(8,128)(2,1)S(1)}, bf16[256,128]{1,0:T(8,128)(2,1)}, u32[]{:S(2)}) copy-start(bf16[256,128]{1,0:T(8,128)(2,1)} %param.9) | copy-start | bytes 196612
  7.2 182.6 %reduce-scatter.2.cloned.1.call-start = ((), (), s32[]{:S(2)}) async-start(), calls=%async_computation.2 | async-start | bytes 4718592 | tf_op jit(solution)/shard_map/reduce_scatter | solution.py:47
  134.1 0.9 copy-start.7
  134.1 4.3 copy-start.6
  135.1 8.4 %collective-permute-start.6 = (bf16[1,128,1024]{2,1,0:T(8,128)(2,1)S(1)}, bf16[1,128,1024]{2,1,0:T(8,128)(2,1)S(1)}, u32[]{:S(2)}, u32[]{:S(2)}) collective-permute-start(bf16[1,128,1024]{2,1,0:T(8,128)(2,1)S(1)} %copy-done.7), channel_id=1, source_target_pairs={{0,8},{8,0},{16,24},{24,16},{32,40},{40,32},{48,56},{56,48},{64,72... | collective-permute-start | bytes 786440 | tf_op jit(solution)/shard_map/ppermute | solution.py:23
  138.4 10.8 %collective-permute-start.3 = (bf16[1,128,1024]{2,1,0:T(8,128)(2,1)S(1)}, bf16[1,128,1024]{2,1,0:T(8,128)(2,1)S(1)}, u32[]{:S(2)}, u32[]{:S(2)}) collective-permute-start(bf16[1,128,1024]{2,1,0:T(8,128)(2,1)S(1)} %copy-done.6), channel_id=1, source_target_pairs={{0,8},{8,0},{16,24},{24,16},{32,40},{40,32},{48,56},{56,48},{64,72... | collective-permute-start | bytes 786440 | tf_op jit(solution)/shard_map/ppermute | solution.py:23
  143.5 52.3 %collective-permute-start.7 = (bf16[1,256,1024]{2,1,0:T(8,128)(2,1)S(1)}, bf16[1,256,1024]{2,1,0:T(8,128)(2,1)S(1)}, u32[]{:S(2)}, u32[]{:S(2)}) collective-permute-start(bf16[1,256,1024]{2,1,0:T(8,128)(2,1)S(1)} %constant_dynamic-update-slice_fusion.8), channel_id=1, source_target_pairs={{0,16},{8,24},{16,0},{24,8},{32,48},{40,56},{48,32},{56,40},{64,80... | collective-permute-start | bytes 1572872 | tf_op jit(solution)/shard_map/ppermute | solution.py:23
  149.2 58.8 %collective-permute-start.4 = (bf16[1,256,1024]{2,1,0:T(8,128)(2,1)S(1)}, bf16[1,256,1024]{2,1,0:T(8,128)(2,1)S(1)}, u32[]{:S(2)}, u32[]{:S(2)}) collective-permute-start(bf16[1,256,1024]{2,1,0:T(8,128)(2,1)S(1)} %constant_dynamic-update-slice_fusion.12), channel_id=1, source_target_pairs={{0,16},{8,24},{16,0},{24,8},{32,48},{40,56},{48,32},{56,40},{64,80... | collective-permute-start | bytes 1572872 | tf_op jit(solution)/shard_map/ppermute | solution.py:23
  192.5 10.2 %collective-permute-start = (bf16[1,1024,128]{2,1,0:T(8,128)(2,1)}, bf16[1,1024,128]{2,1,0:T(8,128)(2,1)}, u32[]{:S(2)}, u32[]{:S(2)}) collective-permute-start(bf16[1,1024,128]{2,1,0:T(8,128)(2,1)} %get-tuple-element.10), channel_id=1, source_target_pairs={{0,8},{8,0},{16,24},{24,16},{32,40},{40,32},{48,56},{56,48},{64,72... | collective-permute-start | bytes 786440 | tf_op jit(solution)/shard_map/ppermute | solution.py:23
  195.8 127.3 %collective-permute-start.8 = (bf16[1,512,1024]{2,1,0:T(8,128)(2,1)S(1)}, bf16[1,512,1024]{2,1,0:T(8,128)(2,1)}, u32[]{:S(2)}, u32[]{:S(2)}) collective-permute-start(bf16[1,512,1024]{2,1,0:T(8,128)(2,1)S(1)} %constant_dynamic-update-slice_fusion.6), channel_id=1, source_target_pairs={{0,32},{8,40},{16,48},{24,56},{32,0},{40,8},{48,16},{56,24},{64,96... | collective-permute-start | bytes 3145736 | tf_op jit(solution)/shard_map/ppermute | solution.py:23
  204.3 112.8 %collective-permute-start.1 = (bf16[1,1024,256]{2,1,0:T(8,128)(2,1)}, bf16[1,1024,256]{2,1,0:T(8,128)(2,1)S(1)}, u32[]{:S(2)}, u32[]{:S(2)}) collective-permute-start(bf16[1,1024,256]{2,1,0:T(8,128)(2,1)} %constant_dynamic-update-slice_fusion.18), channel_id=1, source_target_pairs={{0,16},{8,24},{16,0},{24,8},{32,48},{40,56},{48,32},{56,40},{64,80... | collective-permute-start | bytes 1572872 | tf_op jit(solution)/shard_map/ppermute | solution.py:23
  208.1 116.5 %collective-permute-start.5 = (bf16[1,512,1024]{2,1,0:T(8,128)(2,1)S(1)}, bf16[1,512,1024]{2,1,0:T(8,128)(2,1)}, u32[]{:S(2)}, u32[]{:S(2)}) collective-permute-start(bf16[1,512,1024]{2,1,0:T(8,128)(2,1)S(1)} %constant_dynamic-update-slice_fusion.10), channel_id=1, source_target_pairs={{0,32},{8,40},{16,48},{24,56},{32,0},{40,8},{48,16},{56,24},{64,96... | collective-permute-start | bytes 3145736 | tf_op jit(solution)/shard_map/ppermute | solution.py:23
  317.2 53.1 %collective-permute-start.2 = (bf16[1,1024,512]{2,1,0:T(8,128)(2,1)S(1)}, bf16[1,1024,512]{2,1,0:T(8,128)(2,1)}, u32[]{:S(2)}, u32[]{:S(2)}) collective-permute-start(bf16[1,1024,512]{2,1,0:T(8,128)(2,1)S(1)} %constant_dynamic-update-slice_fusion.16), channel_id=1, source_target_pairs={{0,32},{8,40},{16,48},{24,56},{32,0},{40,8},{48,16},{56,24},{64,96... | collective-permute-start | bytes 3145736 | tf_op jit(solution)/shard_map/ppermute | solution.py:23
  324.5 2.4 copy-start.1
  326.6 1.3 copy-start.2
  377.1 42.1 %copy-start.5 = (f32[1,128,1024]{2,1,0:T(8,128)S(1)}, f32[1,128,1024]{2,1,0:T(8,128)}, u32[]{:S(2)}) copy-start(f32[1,128,1024]{2,1,0:T(8,128)} %param.10) | copy-start | bytes 1572868
  377.1 9.0 %collective-permute-start.9 = (bf16[1,1024,128]{2,1,0:T(8,128)(2,1)S(1)}, bf16[1,1024,128]{2,1,0:T(8,128)(2,1)S(1)}, u32[]{:S(2)}, u32[]{:S(2)}) collective-permute-start(bf16[1,1024,128]{2,1,0:T(8,128)(2,1)S(1)} %get-tuple-element.6), channel_id=1, source_target_pairs={{0,8},{8,0},{16,24},{24,16},{32,40},{40,32},{48,56},{56,48},{64,72... | collective-permute-start | bytes 786440 | tf_op jit(solution)/shard_map/ppermute | solution.py:23
  386.2 27.9 %collective-permute-start.10 = (bf16[1,1024,256]{2,1,0:T(8,128)(2,1)S(1)}, bf16[1,1024,256]{2,1,0:T(8,128)(2,1)S(1)}, u32[]{:S(2)}, u32[]{:S(2)}) collective-permute-start(bf16[1,1024,256]{2,1,0:T(8,128)(2,1)S(1)} %constant_dynamic-update-slice_fusion.2), channel_id=1, source_target_pairs={{0,16},{8,24},{16,0},{24,8},{32,48},{40,56},{48,32},{56,40},{64,80... | collective-permute-start | bytes 1572872 | tf_op jit(solution)/shard_map/ppermute | solution.py:23
  389.1 31.7 %copy-start.3 = (f32[1024,128]{1,0:T(8,128)S(1)}, f32[1024,128]{1,0:T(8,128)}, u32[]{:S(2)}) copy-start(f32[1024,128]{1,0:T(8,128)} %reduce-scatter.2.cloned.1.call-done) | copy-start | bytes 1572868
  389.1 31.7 %copy-start.4 = (f32[1,128,1024]{2,1,0:T(8,128)S(1)}, f32[1,128,1024]{2,1,0:T(8,128)}, u32[]{:S(2)}) copy-start(f32[1,128,1024]{2,1,0:T(8,128)} %param.11) | copy-start | bytes 1572868
  414.1 53.3 %collective-permute-start.11 = (bf16[1,1024,512]{2,1,0:T(8,128)(2,1)S(1)}, bf16[1,1024,512]{2,1,0:T(8,128)(2,1)S(1)}, u32[]{:S(2)}, u32[]{:S(2)}) collective-permute-start(bf16[1,1024,512]{2,1,0:T(8,128)(2,1)S(1)} %constant_dynamic-update-slice_fusion), channel_id=1, source_target_pairs={{0,32},{8,40},{16,48},{24,56},{32,0},{40,8},{48,16},{56,24},{64,96... | collective-permute-start | bytes 3145736 | tf_op jit(solution)/shard_map/ppermute | solution.py:23
Sparse Core Ops, SparseCore 0:
  134.3 55.4 reduce-scatter.1
